TPU v7x, 256 devices: a whole 4x4x8 slice. The times are simulated.
256 devices in a mesh: samp: 32 (over z, x_lo, core), snp: 8 (over x_hi, y).
Axes of the slice: x: 4 (x_hi: 2, x_lo: 2; x = x_hi * 2 + x_lo), y: 4, z: 8, core: 2. Of those that a mesh axis runs over, the one named last changes fastest.
Arguments:
- genotypes: int32 [131072, 4096], P('samp', 'snp'), may hold values from 0 to 2, as said below
- allele_freq: float32 [4096], P('snp'), may hold values from 0.05 to 0.5
- snp_bins: int32 [4096], P('snp'), may hold values from 0 to 11, as said below
- probes: bfloat16 [64, 131072], P(None, 'samp'), may hold values from -6 to 6
- variances: float32 [13], replicated, may hold values from 0.1 to 1
Outputs:
- projected: float32 [131072, 768], P(('samp', 'snp'))
- combined: float32 [64, 131072], P(None, ('samp', 'snp'))
Inputs may be any that keep to these rules, and one draw needn't show every extreme that they name: `genotypes`: dosages 0, 1 or 2. `snp_bins`: every component has at least one SNP.
All inputs are finite; a program needn't handle non-finite values.
Results may differ from a plain program's by a relative error of at most 0.0065.
Values may be sent and summed in bfloat16 or wider, within the bound.
No kernel may reach another device: no remote copies, remote signals or barrier semaphores. Data moves between devices by JAX's collectives and lax.ppermute only.
A program may use at most 128 MiB of HBM per device.

v0:
```python
import jax
import jax.numpy as jnp
from jax import lax
from jax.sharding import PartitionSpec as P

COMPONENTS = 12


def gathered_total(shard, axis):
    return lax.all_gather(shard, axis).sum(0)


def copy_for_each(shard, axis):
    copies = jnp.broadcast_to(shard, (lax.axis_size(axis), *shard.shape))
    return lax.all_to_all(copies, axis, split_axis=0, concat_axis=0, tiled=True)


def in_order(pieces, dim):
    lengths = list(pieces.shape[1:])
    lengths[dim] *= pieces.shape[0]
    return jnp.moveaxis(pieces, 0, dim).reshape(lengths)


def gather_directly(shard, axis, dim):
    pieces = copy_for_each(shard, axis)
    return in_order(pieces, dim)


def standardize(dosage_block, allele_freq):
    spread = jnp.sqrt(2.0 * allele_freq * (1.0 - allele_freq))
    return ((dosage_block.astype(jnp.float32) - 2.0 * allele_freq) / spread).astype(jnp.bfloat16)


def build_weights(scores, snp_bins, counts, labels):
    onehot = (snp_bins[:, None] == labels[None, :]).astype(jnp.float32)
    factor = jnp.sum(onehot * lax.rsqrt(counts)[None, :], 1)
    width = scores.shape[0]
    spread_out = (scores.T * factor[:, None])[:, None, :] * onehot[:, :, None]
    return spread_out.reshape(snp_bins.shape[0], labels.shape[0] * width).astype(jnp.bfloat16)


def body(genotypes, allele_freq, snp_bins, probes, variances):
    standard = standardize(genotypes, allele_freq)
    partial_scores = jnp.dot(probes, standard, preferred_element_type=jnp.float32)
    whole_rows = standard.shape[0] * lax.axis_size("samp")
    scores = gathered_total(partial_scores, "samp") / jnp.sqrt(jnp.float32(whole_rows))
    groups = lax.axis_size("snp")
    own_rows = standard.shape[0] // groups
    snp_index = lax.axis_index("snp")
    labels = jnp.arange(COMPONENTS, dtype=jnp.int32)
    sample_rows = lax.all_to_all(standard, "snp", split_axis=0, concat_axis=1, tiled=True)
    packed = jnp.concatenate([scores, snp_bins.astype(jnp.float32)[None, :]], 0)
    gathered = gather_directly(packed, "snp", 1)
    scores_full = gathered[:-1]
    bins_full = gathered[-1].astype(jnp.int32)
    all_hits = (bins_full[:, None] == labels[None, :]).astype(jnp.float32)
    counts = jnp.sum(all_hits, 0)
    weights = build_weights(scores_full, bins_full, counts, labels)
    projected = jnp.dot(sample_rows, weights, preferred_element_type=jnp.float32)
    width = probes.shape[0]
    stacked = projected.reshape(own_rows, COMPONENTS, width)
    own_probes = lax.dynamic_slice_in_dim(probes, snp_index * own_rows, own_rows, 1).astype(
        jnp.float32
    )
    combined = (
        jnp.einsum("nmb,m->bn", stacked, variances[:COMPONENTS])
        + variances[COMPONENTS] * own_probes
    )
    return (projected, combined)


def solution(mesh):
    placed = (P("samp", "snp"), P("snp"), P("snp"), P(None, "samp"), P())
    return jax.shard_map(
        body,
        mesh=mesh,
        in_specs=placed,
        out_specs=(P(("samp", "snp"), None), P(None, ("samp", "snp"))),
        check_vma=False,
    )
```

profile of v0, /device:TPU:224, one launch (start us, length us, event | category | flops | bytes accessed | tf_op | source)
XLA Modules:
  0.0 145.6 jit_solution(5224861372201181732)
XLA Ops:
  7.2 0.0 all-gather.3.cloned.1.call-start
  7.2 0.7 broadcast_multiply_fusion.1
  7.9 4.6 %divide_convert_fusion = bf16[4096,512]{1,0:T(8,128)(2,1)S(1)} fusion(s32[4096,512]{1,0:T(8,128)} %param.5, f32[512]{0:T(512)S(1)} %get-tuple-element.3, f32[512]{0:T(512)S(1)} %get-tuple-element.2), kind=kLoop, calls=%fused_computation.1 | loop fusion | flops 8388608 | bytes 12587008 | tf_op jit(solution)/shard_map/convert_element_type | solution.py:31
  12.5 0.0 copy-start
  12.6 2.0 %copy-done = bf16[4096,512]{1,0:T(8,128)(2,1)} copy-done((bf16[4096,512]{1,0:T(8,128)(2,1)}, bf16[4096,512]{1,0:T(8,128)(2,1)S(1)}, u32[]{:S(2)}) %copy-start) | copy-done | bytes 4194328
  14.5 1.5 %convolution_bitcast_fusion = f32[64,512]{1,0:T(8,128)} fusion(bf16[64,4096]{1,0:T(8,128)(2,1)S(1)} %copy-done.3, bf16[4096,512]{1,0:T(8,128)(2,1)S(1)} %divide_convert_fusion), kind=kOutput, calls=%fused_computation.4 | convolution fusion | flops 268435456 | bytes 4849664 | tf_op jit(solution)/shard_map/dot_general | solution.py:44
  16.0 0.0 all-gather.3.cloned.1.call-update
  16.0 6.9 %all-to-all-start = ((bf16[8,512,512]{2,1,0:T(8,128)(2,1)}), bf16[8,512,512]{2,1,0:T(8,128)(2,1)}, u32[]{:S(2)}, u32[]{:S(2)}) async-start(bf16[8,512,512]{2,1,0:T(8,128)(2,1)} %bitcast.28), calls=%async_computation | async-start | bytes 8388608 | tf_op jit(solution)/shard_map/all_to_all | solution.py:51
  23.0 0.0 copy-start.5
  23.0 58.5 %all-gather.3.cloned.1.call-done = f32[2048,512]{1,0:T(8,128)} async-done(((f32[64,512]{1,0:T(8,128)}), f32[2048,512]{1,0:T(8,128)}) %all-gather.3.cloned.1.call-update) | async-done | bytes 4194320 | tf_op jit(solution)/shard_map/all_gather | solution.py:10
  81.5 2.5 %reduce_sum.27 = f32[64,512]{1,0:T(8,128)S(1)} reduce(f32[32,64,512]{2,1,0:T(8,128)} %bitcast.34, f32[]{:T(128)} %constant.4.clone.1), dimensions={0}, to_apply=%region_0.0 | reduce | flops 1015808 | bytes 4325380 | tf_op jit(solution)/shard_map/reduce_sum | solution.py:10
  84.1 8.9 %all-to-all-done = bf16[8,512,512]{2,1,0:T(8,128)(2,1)} async-done(((bf16[8,512,512]{2,1,0:T(8,128)(2,1)}), bf16[8,512,512]{2,1,0:T(8,128)(2,1)}, u32[]{:S(2)}, u32[]{:S(2)}) %all-to-all-start) | async-done | bytes 4194336 | tf_op jit(solution)/shard_map/all_to_all | solution.py:51
  93.0 1.2 broadcast_in_dim.5
  94.1 4.2 %all-to-all-start.1 = ((f32[8,65,512]{2,1,0:T(8,128)}), f32[8,65,512]{2,1,0:T(8,128)S(1)}, u32[]{:S(2)}, u32[]{:S(2)}) async-start(f32[8,65,512]{2,1,0:T(8,128)} %broadcast_in_dim.5), calls=%async_computation.1 | async-start | bytes 2359296 | tf_op jit(solution)/shard_map/all_to_all | solution.py:15
  98.4 0.0 copy-done.5
  98.4 0.7 slice.20
  99.0 6.5 %copy.11 = bf16[512,8,512]{0,2,1:T(8,128)(2,1)} copy(bf16[512,8,512]{2,0,1:T(8,128)(2,1)} %bitcast.1) | data formatting | bytes 8388608 | tf_op jit(solution)/shard_map/all_to_all | solution.py:51
  105.6 8.7 %all-to-all-done.1 = f32[8,65,512]{2,1,0:T(8,128)S(1)} async-done(((f32[8,65,512]{2,1,0:T(8,128)}), f32[8,65,512]{2,1,0:T(8,128)S(1)}, u32[]{:S(2)}, u32[]{:S(2)}) %all-to-all-start.1) | async-done | bytes 1064992 | tf_op jit(solution)/shard_map/all_to_all | solution.py:15
  114.3 0.1 slice_bitcast_fusion
  114.4 0.0 copy-start.1
  114.4 0.2 fusion.3
  114.6 0.1 select_reduce_fusion
  114.7 0.1 copy.16
  114.8 0.1 multiply_bitcast_fusion
  114.9 1.4 multiply_convert_fusion
  116.3 0.3 copy-done.1
  116.6 3.5 %fusion.6 = f32[512,768]{1,0:T(8,128)S(1)} fusion(bf16[512,4096]{0,1:T(8,128)(2,1)S(1)} %bitcast.33, bf16[4096,768]{0,1:T(8,128)(2,1)S(1)} %bitcast.29), kind=kOutput, calls=%fused_computation.19 | convolution fusion | flops 3221225472 | bytes 12058624 | tf_op jit(solution)/shard_map/dot_general | solution.py:59
  120.1 0.0 copy-start.2
  120.1 0.3 copy.13
  120.4 7.1 %fusion = f32[1,512,64]{0,1,2:T(8,128)} fusion(bf16[512,12,64]{0,2,1:T(8,128)(2,1)S(1)} %bitcast.30, f32[13]{0:T(128)S(1)} %copy-done.5), kind=kOutput, calls=%fused_computation.2 | convolution fusion | flops 786432 | bytes 917556 | tf_op jit(solution)/shard_map/nmb,m->bn/dot_general | solution.py:66
  127.4 9.9 %copy.15 = f32[1,512,64]{1,2,0:T(8,128)S(1)} copy(f32[1,512,64]{0,1,2:T(8,128)} %fusion) | data formatting | bytes 262144 | tf_op jit(solution)/shard_map/nmb,m->bn/dot_general | solution.py:66
  137.4 1.4 bitcast_add_fusion
  (11 shorter events, 0.1 us)
Async XLA Ops:
  7.2 74.3 %all-gather.3.cloned.1.call-start = ((), (), s32[]{:S(2)}) async-start(), calls=%async_computation.2 | async-start | bytes 4325376 | tf_op jit(solution)/shard_map/all_gather | solution.py:10
  7.9 6.6 %copy-start.3 = (bf16[64,4096]{1,0:T(8,128)(2,1)S(1)}, bf16[64,4096]{1,0:T(8,128)(2,1)}, u32[]{:S(2)}) copy-start(bf16[64,4096]{1,0:T(8,128)(2,1)} %param.8) | copy-start | bytes 1572868
  12.5 2.0 %copy-start = (bf16[4096,512]{1,0:T(8,128)(2,1)}, bf16[4096,512]{1,0:T(8,128)(2,1)S(1)}, u32[]{:S(2)}) copy-start(bf16[4096,512]{1,0:T(8,128)(2,1)S(1)} %divide_convert_fusion) | copy-start | bytes 12582916
  14.5 8.5 %copy-start.4 = (s32[512]{0:T(512)S(1)}, s32[512]{0:T(512)}, u32[]{:S(2)}) copy-start(s32[512]{0:T(512)} %param.7) | copy-start | bytes 6148
  16.0 76.9 %all-to-all-start = ((bf16[8,512,512]{2,1,0:T(8,128)(2,1)}), bf16[8,512,512]{2,1,0:T(8,128)(2,1)}, u32[]{:S(2)}, u32[]{:S(2)}) async-start(bf16[8,512,512]{2,1,0:T(8,128)(2,1)} %bitcast.28), calls=%async_computation | async-start | bytes 8388608 | tf_op jit(solution)/shard_map/all_to_all | solution.py:51
  23.0 75.4 %copy-start.5 = (f32[13]{0:T(128)S(1)}, f32[13]{0:T(128)}, u32[]{:S(2)}) copy-start(f32[13]{0:T(128)} %param.9) | copy-start | bytes 160
  94.1 20.2 %all-to-all-start.1 = ((f32[8,65,512]{2,1,0:T(8,128)}), f32[8,65,512]{2,1,0:T(8,128)S(1)}, u32[]{:S(2)}, u32[]{:S(2)}) async-start(f32[8,65,512]{2,1,0:T(8,128)} %broadcast_in_dim.5), calls=%async_computation.1 | async-start | bytes 2359296 | tf_op jit(solution)/shard_map/all_to_all | solution.py:15
  114.4 2.2 %copy-start.1 = (bf16[512,8,512]{0,2,1:T(8,128)(2,1)S(1)}, bf16[512,8,512]{0,2,1:T(8,128)(2,1)}, u32[]{:S(2)}) copy-start(bf16[512,8,512]{0,2,1:T(8,128)(2,1)} %copy.11) | copy-start | bytes 12582916
  120.1 7.4 %copy-start.2 = (f32[512,768]{1,0:T(8,128)}, f32[512,768]{1,0:T(8,128)S(1)}, u32[]{:S(2)}) copy-start(f32[512,768]{1,0:T(8,128)S(1)} %fusion.6) | copy-start | bytes 4718596
Sparse Core Ops, SparseCore 0:
  16.2 65.2 all-gather.2
where the time goes:
time: 146 us
  waiting for transfers between devices  76.1 us (52%)
  local copies, waits for them, and re-layouts  21 us (14%)
  between operations  14.2 us (10%)
  matrix products  12 us (8%)
  starting transfers between devices  11.2 us (8%)
  other arithmetic  11.1 us (8%)
    all_gather x1, waiting for transfers between devices, gathered_total(): return lax.all_gather(shard, axis).sum(0)  58.5 us
    dot_general x1, local copies, waits for them, and re-layouts, body(): jnp.einsum('nmb,m->bn', stacked, variances[:COMPONENTS])  9.95 us
    all_to_all x1, waiting for transfers between devices, body(): lax.all_to_all(standard, 'snp', split_axis=0, concat_axis=1, tiled=True)  8.87 us
    all_to_all x1, waiting for transfers between devices, copy_for_each(): return lax.all_to_all(copies, axis, split_axis=0, concat_axis=0, tiled=True)  8.75 us
    dot_general x1, matrix products, body(): jnp.einsum('nmb,m->bn', stacked, variances[:COMPONENTS])  7.08 us
    all_to_all x1, starting transfers between devices, body(): lax.all_to_all(standard, 'snp', split_axis=0, concat_axis=1, tiled=True)  6.94 us
    all_to_all x1, local copies, waits for them, and re-layouts, body(): lax.all_to_all(standard, 'snp', split_axis=0, concat_axis=1, tiled=True)  6.53 us
    convert_element_type x1, other arithmetic, standardize(): ((dosage_block.astype(jnp.float32) - 2.0 * allele_freq) / spread).astype(...  4.64 us
  transfers between devices with their start and end apart: 3, of which 3 were waited for; matrix products, arithmetic and copies ran while one was open for 7% of the time, Pallas kernels for 0%

commit v1 on v0

v1 whole, which is shorter than its diff:
```python
import math

import jax
import jax.numpy as jnp
from jax import lax
from jax.experimental import pallas as pl
from jax.experimental.pallas import tpu as pltpu
from jax.sharding import PartitionSpec as P


COMPONENTS = 12
RING = 4
CORES = 2
SHIFTS = ((1, 0), (0, 1), (0, 3), (1, 1), (1, 3), (0, 2), (1, 2), (0, 0))
STAGES = ((7, 0, 1, 2, 3), (4, 5), (6,))


def standardize_kernel(order_ref, dosage_ref, freq_ref, probes_ref, *outs):
    slots, partial_ref = outs[:-1], outs[-1]
    step = pl.program_id(0)
    freq = freq_ref[...]
    scale = 1.0 / jnp.sqrt(2.0 * freq * (1.0 - freq))
    standard = ((dosage_ref[...].astype(jnp.float32) - 2.0 * freq) * scale).astype(jnp.bfloat16)
    for place, slot in enumerate(slots):

        @pl.when(step == place)
        def _():
            slot[...] = standard

    scores = jnp.dot(probes_ref[...], standard, preferred_element_type=jnp.float32)

    @pl.when(step == 0)
    def _():
        partial_ref[...] = scores

    @pl.when(step > 0)
    def _():
        partial_ref[...] += scores


def standardize_and_score(order, genotypes, allele_freq, probes):
    rows, snps = genotypes.shape
    width = probes.shape[0]
    groups = order.shape[0]
    block = rows // groups
    return pl.pallas_call(
        standardize_kernel,
        grid_spec=pltpu.PrefetchScalarGridSpec(
            num_scalar_prefetch=1,
            grid=(groups,),
            in_specs=[
                pl.BlockSpec((block, snps), lambda i, order: (order[i], 0)),
                pl.BlockSpec((1, snps), lambda i, order: (0, 0)),
                pl.BlockSpec((width, block), lambda i, order: (0, order[i])),
            ],
            out_specs=[pl.BlockSpec((block, snps), lambda i, order: (0, 0))] * groups
            + [pl.BlockSpec((width, snps), lambda i, order: (0, 0))],
        ),
        out_shape=[jax.ShapeDtypeStruct((block, snps), jnp.bfloat16)] * groups
        + [jax.ShapeDtypeStruct((width, snps), jnp.float32)],
    )(order, genotypes, allele_freq[None, :], probes)


def project_kernel(slots, first, last, *refs):
    order_ref, scores_ref, kinds_ref, variances_ref, probes_ref = refs[:5]
    chunk_refs = refs[5 : 5 + len(slots)]
    rest = refs[5 + len(slots) :]
    so_far_ref = None if first else rest[0]
    projected_ref = rest[0 if first else 1]
    kinds_scratch = rest[-1]
    factor_scratch = rest[-2]
    width = scores_ref.shape[1]

    kinds = kinds_ref[...].astype(jnp.float32)
    factor = jnp.zeros_like(kinds)
    for m in range(COMPONENTS):
        hits = kinds == float(m)
        count = jnp.sum(jnp.sum(hits.astype(jnp.float32), 1, keepdims=True), 0, keepdims=True)
        factor = jnp.where(hits, lax.rsqrt(count), factor)
    kinds_scratch[...] = kinds
    factor_scratch[...] = factor

    total = None if first else so_far_ref[...]
    for slot, chunk_ref in zip(slots, chunk_refs):
        source = order_ref[slot]
        kind = kinds_scratch[pl.ds(source, 1), :]
        weighted = scores_ref[source].astype(jnp.float32) * factor_scratch[pl.ds(source, 1), :]
        weights = jnp.concatenate(
            [jnp.where(kind == float(m), weighted, 0.0).astype(jnp.bfloat16) for m in range(COMPONENTS)], 0
        )
        product = lax.dot_general(
            chunk_ref[...], weights, (((1,), (1,)), ((), ())), preferred_element_type=jnp.float32
        )
        total = product if total is None else total + product
    projected_ref[...] = total
    if last:
        mixed = sum(variances_ref[m] * total[:, m * width : (m + 1) * width] for m in range(COMPONENTS))
        rest[2][...] = mixed.T + variances_ref[COMPONENTS] * probes_ref[...].astype(jnp.float32)


def project(stage, order, scores, kinds, variances, own_probes, chunks, so_far):
    slots = STAGES[stage]
    first, last = stage == 0, stage == len(STAGES) - 1
    width, rows = own_probes.shape
    columns = COMPONENTS * width
    whole = pl.BlockSpec(memory_space=pltpu.VMEM)
    scalars = pl.BlockSpec(memory_space=pltpu.SMEM)
    extra = [] if first else [so_far]
    out_shape = [jax.ShapeDtypeStruct((rows, columns), jnp.float32)]
    if last:
        out_shape.append(jax.ShapeDtypeStruct((width, rows), jnp.float32))
    return pl.pallas_call(
        lambda *refs: project_kernel(slots, first, last, *refs),
        in_specs=[scalars, whole, whole, scalars, whole] + [whole] * (len(slots) + len(extra)),
        out_specs=[whole] * len(out_shape),
        out_shape=out_shape,
        scratch_shapes=[pltpu.VMEM(kinds.shape, jnp.float32)] * 2,
    )(order, scores, kinds, variances, own_probes, *[chunks[slot] for slot in slots], *extra)


def exchange(value, axis, target_of):
    return lax.ppermute(value, axis, [(i, target_of(i)) for i in range(lax.axis_size(axis))])


def shifted(index, dx, dy):
    return (index // RING ^ dx) * RING + (index % RING + dy) % RING


def body(genotypes, allele_freq, snp_bins, probes, variances):
    samp, snp = lax.axis_size("samp"), lax.axis_size("snp")
    rows, snps = genotypes.shape
    width = probes.shape[0]
    own_rows = rows // snp
    half = width // CORES
    depth = samp // (2 * CORES)
    core = lax.axis_index("samp") % CORES
    me = lax.axis_index("snp")

    targets = jnp.stack([shifted(me, dx, dy) for dx, dy in SHIFTS]).astype(jnp.int32)
    sources = jnp.stack([shifted(me, dx, RING - dy) for dx, dy in SHIFTS]).astype(jnp.int32)
    *blocks, partial = standardize_and_score(targets, genotypes, allele_freq, probes)
    chunks = [blocks[-1]] * len(SHIFTS)
    for slot, (dx, dy) in enumerate(SHIFTS[:-1]):
        chunks[slot] = exchange(blocks[slot], "snp", lambda i: shifted(i, dx, dy))

    halves = (partial * (1.0 / math.sqrt(rows * samp))).reshape(CORES, half, snps)
    other = exchange(lax.dynamic_index_in_dim(halves, 1 - core, 0, keepdims=False), "samp", lambda i: i ^ 1)
    mine = lax.dynamic_index_in_dim(halves, core, 0, keepdims=False) + other
    flip = 1
    while flip < depth:
        mine = mine + exchange(mine, "samp", lambda i: i ^ (2 * CORES * flip))
        flip *= 2

    tail = jnp.zeros((half, snps // 4), jnp.bfloat16).at[:4].set(snp_bins.astype(jnp.bfloat16).reshape(4, snps // 4))
    packed = jnp.concatenate([mine.astype(jnp.bfloat16), tail], 1)
    planes = [
        [(z * 2 * CORES + lo * CORES + c) * snp + k for lo in range(2) for k in range(snp)]
        for z in range(depth)
        for c in range(CORES)
    ]
    copies = jnp.broadcast_to(packed, (2 * snp, *packed.shape))
    gathered = lax.all_to_all(
        copies, ("samp", "snp"), split_axis=0, concat_axis=0, tiled=True, axis_index_groups=planes
    )
    kinds = gathered[:snp, :4, snps:].reshape(snp, snps)
    mine = (gathered[:snp, :, :snps].astype(jnp.float32) + gathered[snp:, :, :snps].astype(jnp.float32)).astype(jnp.bfloat16)
    other = exchange(mine, "samp", lambda i: i ^ 1)
    scores = jnp.concatenate([jnp.where(core == 0, mine, other), jnp.where(core == 0, other, mine)], 1)

    own_probes = lax.dynamic_slice_in_dim(probes, me * own_rows, own_rows, 1)
    state = [None]
    for stage in range(len(STAGES)):
        state = project(stage, sources, scores, kinds, variances, own_probes, chunks, state[0])
    return tuple(state)


def solution(mesh):
    placed = (P("samp", "snp"), P("snp"), P("snp"), P(None, "samp"), P())
    return jax.shard_map(
        body,
        mesh=mesh,
        in_specs=placed,
        out_specs=(P(("samp", "snp"), None), P(None, ("samp", "snp"))),
        check_vma=False,
    )
```

time: 146 us -> 125 us (0.86)
  the two profiles are of different devices: /device:TPU:224 before, /device:TPU:1 now
where the time goes in v1:
time: 125 us
  waiting for transfers between devices  53.1 us (42%)
  starting transfers between devices  37.5 us (30%)
  Pallas kernels  24 us (19%)
  local copies, waits for them, and re-layouts  6.62 us (5%)
  other arithmetic  2.75 us (2%)
    ppermute x12, waiting for transfers between devices, exchange(): lax.ppermute(value, axis, [(i, target_of(i)) for i in range(lax.axis_size...  47.8 us
    ppermute x12, starting transfers between devices, exchange(): lax.ppermute(value, axis, [(i, target_of(i)) for i in range(lax.axis_size...  30.9 us
    pallas_call x3, Pallas kernels, project(): pl.pallas_call(lambda *refs: project_kernel(slots, first, last, *refs), i...  13.3 us
    pallas_call x1, Pallas kernels, standardize_and_score(): pl.pallas_call(standardize_kernel, grid_spec=pltpu.PrefetchScalarGridSpec...  10.7 us
    all_to_all x1, starting transfers between devices, body(): lax.all_to_all(copies, ('samp', 'snp'), split_axis=0, concat_axis=0, tile...  6.6 us
    all_to_all x1, waiting for transfers between devices, body(): lax.all_to_all(copies, ('samp', 'snp'), split_axis=0, concat_axis=0, tile...  5.33 us
    unnamed x16, local copies, waits for them, and re-layouts  3 us
  transfers between devices with their start and end apart: 13, of which 6 were waited for; matrix products, arithmetic and copies ran while one was open for 4% of the time, Pallas kernels for 8%

profile of v1, /device:TPU:1, one launch (start us, length us, event | category | flops | bytes accessed | tf_op | source)
XLA Modules:
  0.0 124.8 jit_solution(15853035710942161050)
XLA Ops:
  0.7 0.6 stack.53.order_ref
  1.4 10.7 %shard_map.68 = (bf16[512,512]{1,0:T(8,128)(2,1)}, bf16[512,512]{1,0:T(8,128)(2,1)}, bf16[512,512]{1,0:T(8,128)(2,1)}, bf16[512,512]{1,0:T(8,128)(2,1)}, bf16[51...) custom-call(s32[8]{0:T(128)} %stack.53.order_ref, ...), custom_call_target="tpu_custom_call" | custom-call | tf_op jit(solution)/shard_map/pallas_call | solution.py:46
  12.1 1.0 broadcast_multiply_fusion
  13.1 3.3 %collective-permute-start = (f32[32,512]{1,0:T(8,128)S(1)}, f32[32,512]{1,0:T(8,128)S(1)}, u32[]{:S(2)}, u32[]{:S(2)}) collective-permute-start(f32[32,512]{1,0:T(8,128)S(1)} %dynamic-slice_bitcast_fusion), channel_id=1, source_target_pairs={{0,8},{8,0},{16,24},{24,16},{32,40},{40,32},{48,56},{56,48},{64,72... | collective-permute-start | bytes 196616 | tf_op jit(solution)/shard_map/ppermute | solution.py:122
  16.4 0.9 collective-permute-done
  17.4 3.1 %collective-permute-done.1 = f32[32,512]{1,0:T(8,128)S(1)} collective-permute-done((f32[32,512]{1,0:T(8,128)S(1)}, f32[32,512]{1,0:T(8,128)S(1)}, u32[]{:S(2)}, u32[]{:S(2)}) %collective-permute-start.1) | collective-permute-done | bytes 65568 | tf_op jit(solution)/shard_map/ppermute | solution.py:122
  20.5 1.9 %collective-permute-start.2 = (f32[32,512]{1,0:T(8,128)S(1)}, f32[32,512]{1,0:T(8,128)S(1)}, u32[]{:S(2)}, u32[]{:S(2)}) collective-permute-start(f32[32,512]{1,0:T(8,128)S(1)} %add.161), channel_id=1, source_target_pairs={{0,64},{8,72},{16,80},{24,88},{32,96},{40,104},{48,112},{56,120},{... | collective-permute-start | bytes 196616 | tf_op jit(solution)/shard_map/ppermute | solution.py:122
  22.4 2.9 %collective-permute-done.2 = f32[32,512]{1,0:T(8,128)S(1)} collective-permute-done((f32[32,512]{1,0:T(8,128)S(1)}, f32[32,512]{1,0:T(8,128)S(1)}, u32[]{:S(2)}, u32[]{:S(2)}) %collective-permute-start.2) | collective-permute-done | bytes 65568 | tf_op jit(solution)/shard_map/ppermute | solution.py:122
  25.3 5.3 %collective-permute-start.3 = (f32[32,512]{1,0:T(8,128)S(1)}, f32[32,512]{1,0:T(8,128)S(1)}, u32[]{:S(2)}, u32[]{:S(2)}) collective-permute-start(f32[32,512]{1,0:T(8,128)S(1)} %add.162), channel_id=1, source_target_pairs={{0,128},{8,136},{16,144},{24,152},{32,160},{40,168},{48,176},{56,1... | collective-permute-start | bytes 196616 | tf_op jit(solution)/shard_map/ppermute | solution.py:122
  30.6 1.8 %collective-permute-done.3 = f32[32,512]{1,0:T(8,128)S(1)} collective-permute-done((f32[32,512]{1,0:T(8,128)S(1)}, f32[32,512]{1,0:T(8,128)S(1)}, u32[]{:S(2)}, u32[]{:S(2)}) %collective-permute-start.3) | collective-permute-done | bytes 65568 | tf_op jit(solution)/shard_map/ppermute | solution.py:122
  32.5 0.9 broadcast_in_dim.8
  33.3 6.6 %all-to-all-start = ((bf16[16,32,640]{2,1,0:T(8,128)(2,1)}), bf16[16,32,640]{2,1,0:T(8,128)(2,1)S(1)}, u32[]{:S(2)}, u32[]{:S(2)}) async-start(bf16[16,32,640]{2,1,0:T(8,128)(2,1)} %broadcast_in_dim.8), calls=%async_computation | async-start | bytes 1310720 | tf_op jit(solution)/shard_map/all_to_all | solution.py:162
  40.0 3.0 %collective-permute-start.8 = (bf16[512,512]{1,0:T(8,128)(2,1)S(1)}, bf16[512,512]{1,0:T(8,128)(2,1)S(1)}, u32[]{:S(2)}, u32[]{:S(2)}) collective-permute-start(bf16[512,512]{1,0:T(8,128)(2,1)S(1)} %copy-done.6), channel_id=1, source_target_pairs={{0,4},{1,5},{2,6},{3,7},{4,0},{5,1},{6,2},{7,3},{8,12},{9,13},{10,... | collective-permute-start | bytes 1572872 | tf_op jit(solution)/shard_map/ppermute | solution.py:122
  42.9 1.2 collective-permute-start.9
  44.1 5.3 %all-to-all-done = bf16[16,32,640]{2,1,0:T(8,128)(2,1)S(1)} async-done(((bf16[16,32,640]{2,1,0:T(8,128)(2,1)}), bf16[16,32,640]{2,1,0:T(8,128)(2,1)S(1)}, u32[]{:S(2)}, u32[]{:S(2)}) %all-to-all-start) | async-done | bytes 655392 | tf_op jit(solution)/shard_map/all_to_all | solution.py:162
  49.4 0.8 add_convert_fusion
  50.2 7.9 %collective-permute-start.4 = (bf16[8,32,512]{2,1,0:T(8,128)(2,1)}, bf16[8,32,512]{2,1,0:T(8,128)(2,1)S(1)}, u32[]{:S(2)}, u32[]{:S(2)}) collective-permute-start(bf16[8,32,512]{2,1,0:T(8,128)(2,1)} %add_convert_fusion), channel_id=1, source_target_pairs={{0,8},{8,0},{16,24},{24,16},{32,40},{40,32},{48,56},{56,48},{64,72... | collective-permute-start | bytes 786440 | tf_op jit(solution)/shard_map/ppermute | solution.py:122
  58.1 1.4 %collective-permute-start.5 = (bf16[512,512]{1,0:T(8,128)(2,1)}, bf16[512,512]{1,0:T(8,128)(2,1)S(1)}, u32[]{:S(2)}, u32[]{:S(2)}) collective-permute-start(bf16[512,512]{1,0:T(8,128)(2,1)} %get-tuple-element.24), channel_id=1, source_target_pairs={{0,6},{1,7},{2,4},{3,5},{4,2},{5,3},{6,0},{7,1},{8,14},{9,15},{10,... | collective-permute-start | bytes 1572872 | tf_op jit(solution)/shard_map/ppermute | solution.py:122
  59.5 3.3 %collective-permute-start.6 = (bf16[512,512]{1,0:T(8,128)(2,1)}, bf16[512,512]{1,0:T(8,128)(2,1)S(1)}, u32[]{:S(2)}, u32[]{:S(2)}) collective-permute-start(bf16[512,512]{1,0:T(8,128)(2,1)} %get-tuple-element.25), channel_id=1, source_target_pairs={{0,7},{1,4},{2,5},{3,6},{4,3},{5,0},{6,1},{7,2},{8,15},{9,12},{10,... | collective-permute-start | bytes 1572872 | tf_op jit(solution)/shard_map/ppermute | solution.py:122
  62.8 0.6 stack.50.refs_0_
  63.4 1.5 %constant_dynamic-slice_fusion.refs_4_ = bf16[64,512]{1,0:T(8,128)(2,1)} fusion(bf16[64,4096]{1,0:T(8,128)(2,1)} %probes_ref.1, s32[]{:T(128)S(6)} %select_n.137), kind=kLoop, calls=%fused_computation.14 | loop fusion | bytes 131076 | tf_op jit(solution)/shard_map/dynamic_slice | solution.py:170
  64.9 1.5 %collective-permute-start.7 = (bf16[512,512]{1,0:T(8,128)(2,1)}, bf16[512,512]{1,0:T(8,128)(2,1)S(1)}, u32[]{:S(2)}, u32[]{:S(2)}) collective-permute-start(bf16[512,512]{1,0:T(8,128)(2,1)} %get-tuple-element.26), channel_id=1, source_target_pairs={{0,2},{1,3},{2,0},{3,1},{4,6},{5,7},{6,4},{7,5},{8,10},{9,11},{10,... | collective-permute-start | bytes 1572872 | tf_op jit(solution)/shard_map/ppermute | solution.py:122
  66.4 2.1 %collective-permute-start.10 = (bf16[512,512]{1,0:T(8,128)(2,1)}, bf16[512,512]{1,0:T(8,128)(2,1)}, u32[]{:S(2)}, u32[]{:S(2)}) collective-permute-start(bf16[512,512]{1,0:T(8,128)(2,1)} %get-tuple-element.30), channel_id=1, source_target_pairs={{0,3},{1,0},{2,1},{3,2},{4,7},{5,4},{6,5},{7,6},{8,11},{9,8},{10,9... | collective-permute-start | bytes 1572872 | tf_op jit(solution)/shard_map/ppermute | solution.py:122
  68.5 0.6 copy.9
  69.2 0.8 pad_maximum_fusion.refs_1_
  70.1 39.0 %collective-permute-done.10.refs_8_ = bf16[512,512]{1,0:T(8,128)(2,1)} collective-permute-done((bf16[512,512]{1,0:T(8,128)(2,1)}, bf16[512,512]{1,0:T(8,128)(2,1)}, u32[]{:S(2)}, u32[]{:S(2)}) %collective-permute-start.10) | collective-permute-done | bytes 524320 | tf_op jit(solution)/shard_map/ppermute | solution.py:122
  109.1 5.4 %shard_map.69.refs_7_ = f32[512,768]{1,0:T(8,128)} custom-call(s32[8]{0:T(128)} %stack.50.refs_0_, bf16[8,64,512]{2,1,0:T(8,128)(2,1)} %pad_maximum_fusion.refs_1_, bf16[8,512]{1,0:T(8,128)(2,1)} %bitcast.25, f32[13]{0:T(128)} %refs_3_.5, bf16[64,512]{1,0:T(8,128)(2,1)} %constant_dynamic-slice_fusion.refs_4_, bf16[512,512]{1,0:T(8,128)(2,1)} %get-tuple-element.27.refs_5_, ...), custom_call_target="tpu_custom_call" | custom-call | tf_op jit(solution)/shard_map/pallas_call | solution.py:112
  114.5 0.8 copy-done.3
  115.3 0.8 copy-done.4
  116.1 4.2 %shard_map.70.refs_6_ = f32[512,768]{1,0:T(8,128)} custom-call(s32[8]{0:T(128)} %stack.50.refs_0_, bf16[8,64,512]{2,1,0:T(8,128)(2,1)} %pad_maximum_fusion.refs_1_, bf16[8,512]{1,0:T(8,128)(2,1)} %bitcast.26, f32[13]{0:T(128)} %refs_3_.5, bf16[64,512]{1,0:T(8,128)(2,1)} %constant_dynamic-slice_fusion.refs_4_, bf16[512,512]{1,0:T(8,128)(2,1)} %copy-done.3, ...), custom_call_target="tpu_custom_call" | custom-call | tf_op jit(solution)/shard_map/pallas_call | solution.py:112
  120.3 0.8 copy-done
  121.1 3.7 %shard_map.71 = (f32[512,768]{1,0:T(8,128)}, f32[64,512]{1,0:T(8,128)}) custom-call(s32[8]{0:T(128)} %stack.50.refs_0_, bf16[8,64,512]{2,1,0:T(8,128)(2,1)} %pad_maximum_fusion.refs_1_, bf16[8,512]{1,0:T(8,128)(2,1)} %bitcast.27, f32[13]{0:T(128)} %refs_3_.5, bf16[64,512]{1,0:T(8,128)(2,1)} %constant_dynamic-slice_fusion.refs_4_, bf16[512,512]{1,0:T(8,128)(2,1)} %copy-done, ...), custom_call_target="tpu_custom_call" | custom-call | tf_op jit(solution)/shard_map/pallas_call | solution.py:112
  (29 shorter events, 0.3 us)
Async XLA Ops:
  1.4 29.3 %copy-start.5 = (s32[512]{0:T(512)S(1)}, s32[512]{0:T(512)}, u32[]{:S(2)}) copy-start(s32[512]{0:T(512)} %param.9) | copy-start | bytes 6148
  12.1 27.9 %copy-start.6 = (bf16[512,512]{1,0:T(8,128)(2,1)S(1)}, bf16[512,512]{1,0:T(8,128)(2,1)}, u32[]{:S(2)}) copy-start(bf16[512,512]{1,0:T(8,128)(2,1)} %get-tuple-element.28) | copy-start | bytes 1572868
  13.1 4.2 %collective-permute-start = (f32[32,512]{1,0:T(8,128)S(1)}, f32[32,512]{1,0:T(8,128)S(1)}, u32[]{:S(2)}, u32[]{:S(2)}) collective-permute-start(f32[32,512]{1,0:T(8,128)S(1)} %dynamic-slice_bitcast_fusion), channel_id=1, source_target_pairs={{0,8},{8,0},{16,24},{24,16},{32,40},{40,32},{48,56},{56,48},{64,72... | collective-permute-start | bytes 196616 | tf_op jit(solution)/shard_map/ppermute | solution.py:122
  17.3 3.2 %collective-permute-start.1 = (f32[32,512]{1,0:T(8,128)S(1)}, f32[32,512]{1,0:T(8,128)S(1)}, u32[]{:S(2)}, u32[]{:S(2)}) collective-permute-start(f32[32,512]{1,0:T(8,128)S(1)} %bitcast_add_fusion), channel_id=1, source_target_pairs={{0,32},{8,40},{16,48},{24,56},{32,0},{40,8},{48,16},{56,24},{64,96... | collective-permute-start | bytes 196616 | tf_op jit(solution)/shard_map/ppermute | solution.py:122
  20.5 4.8 %collective-permute-start.2 = (f32[32,512]{1,0:T(8,128)S(1)}, f32[32,512]{1,0:T(8,128)S(1)}, u32[]{:S(2)}, u32[]{:S(2)}) collective-permute-start(f32[32,512]{1,0:T(8,128)S(1)} %add.161), channel_id=1, source_target_pairs={{0,64},{8,72},{16,80},{24,88},{32,96},{40,104},{48,112},{56,120},{... | collective-permute-start | bytes 196616 | tf_op jit(solution)/shard_map/ppermute | solution.py:122
  25.3 7.1 %collective-permute-start.3 = (f32[32,512]{1,0:T(8,128)S(1)}, f32[32,512]{1,0:T(8,128)S(1)}, u32[]{:S(2)}, u32[]{:S(2)}) collective-permute-start(f32[32,512]{1,0:T(8,128)S(1)} %add.162), channel_id=1, source_target_pairs={{0,128},{8,136},{16,144},{24,152},{32,160},{40,168},{48,176},{56,1... | collective-permute-start | bytes 196616 | tf_op jit(solution)/shard_map/ppermute | solution.py:122
  33.3 16.1 %all-to-all-start = ((bf16[16,32,640]{2,1,0:T(8,128)(2,1)}), bf16[16,32,640]{2,1,0:T(8,128)(2,1)S(1)}, u32[]{:S(2)}, u32[]{:S(2)}) async-start(bf16[16,32,640]{2,1,0:T(8,128)(2,1)} %broadcast_in_dim.8), calls=%async_computation | async-start | bytes 1310720 | tf_op jit(solution)/shard_map/all_to_all | solution.py:162
  40.0 25.0 %collective-permute-start.8 = (bf16[512,512]{1,0:T(8,128)(2,1)S(1)}, bf16[512,512]{1,0:T(8,128)(2,1)S(1)}, u32[]{:S(2)}, u32[]{:S(2)}) collective-permute-start(bf16[512,512]{1,0:T(8,128)(2,1)S(1)} %copy-done.6), channel_id=1, source_target_pairs={{0,4},{1,5},{2,6},{3,7},{4,0},{5,1},{6,2},{7,3},{8,12},{9,13},{10,... | collective-permute-start | bytes 1572872 | tf_op jit(solution)/shard_map/ppermute | solution.py:122
  42.9 23.5 %collective-permute-start.9 = (bf16[512,512]{1,0:T(8,128)(2,1)}, bf16[512,512]{1,0:T(8,128)(2,1)S(1)}, u32[]{:S(2)}, u32[]{:S(2)}) collective-permute-start(bf16[512,512]{1,0:T(8,128)(2,1)} %get-tuple-element.29), channel_id=1, source_target_pairs={{0,1},{1,2},{2,3},{3,0},{4,5},{5,6},{6,7},{7,4},{8,9},{9,10},{10,1... | collective-permute-start | bytes 1572872 | tf_op jit(solution)/shard_map/ppermute | solution.py:122
  50.2 18.3 %collective-permute-start.4 = (bf16[8,32,512]{2,1,0:T(8,128)(2,1)}, bf16[8,32,512]{2,1,0:T(8,128)(2,1)S(1)}, u32[]{:S(2)}, u32[]{:S(2)}) collective-permute-start(bf16[8,32,512]{2,1,0:T(8,128)(2,1)} %add_convert_fusion), channel_id=1, source_target_pairs={{0,8},{8,0},{16,24},{24,16},{32,40},{40,32},{48,56},{56,48},{64,72... | collective-permute-start | bytes 786440 | tf_op jit(solution)/shard_map/ppermute | solution.py:122
  58.1 62.3 %collective-permute-start.5 = (bf16[512,512]{1,0:T(8,128)(2,1)}, bf16[512,512]{1,0:T(8,128)(2,1)S(1)}, u32[]{:S(2)}, u32[]{:S(2)}) collective-permute-start(bf16[512,512]{1,0:T(8,128)(2,1)} %get-tuple-element.24), channel_id=1, source_target_pairs={{0,6},{1,7},{2,4},{3,5},{4,2},{5,3},{6,0},{7,1},{8,14},{9,15},{10,... | collective-permute-start | bytes 1572872 | tf_op jit(solution)/shard_map/ppermute | solution.py:122
  59.5 55.0 %collective-permute-start.6 = (bf16[512,512]{1,0:T(8,128)(2,1)}, bf16[512,512]{1,0:T(8,128)(2,1)S(1)}, u32[]{:S(2)}, u32[]{:S(2)}) collective-permute-start(bf16[512,512]{1,0:T(8,128)(2,1)} %get-tuple-element.25), channel_id=1, source_target_pairs={{0,7},{1,4},{2,5},{3,6},{4,3},{5,0},{6,1},{7,2},{8,15},{9,12},{10,... | collective-permute-start | bytes 1572872 | tf_op jit(solution)/shard_map/ppermute | solution.py:122
  64.9 44.2 %copy-start.1 = (bf16[512,512]{1,0:T(8,128)(2,1)}, bf16[512,512]{1,0:T(8,128)(2,1)S(1)}, u32[]{:S(2)}) copy-start(bf16[512,512]{1,0:T(8,128)(2,1)S(1)} %collective-permute-done.8.refs_6_) | copy-start | bytes 1572868
  64.9 49.6 %collective-permute-start.7 = (bf16[512,512]{1,0:T(8,128)(2,1)}, bf16[512,512]{1,0:T(8,128)(2,1)S(1)}, u32[]{:S(2)}, u32[]{:S(2)}) collective-permute-start(bf16[512,512]{1,0:T(8,128)(2,1)} %get-tuple-element.26), channel_id=1, source_target_pairs={{0,2},{1,3},{2,0},{3,1},{4,6},{5,7},{6,4},{7,5},{8,10},{9,11},{10,... | collective-permute-start | bytes 1572872 | tf_op jit(solution)/shard_map/ppermute | solution.py:122
  66.4 42.7 %copy-start.2 = (bf16[512,512]{1,0:T(8,128)(2,1)}, bf16[512,512]{1,0:T(8,128)(2,1)S(1)}, u32[]{:S(2)}) copy-start(bf16[512,512]{1,0:T(8,128)(2,1)S(1)} %collective-permute-done.9.refs_7_) | copy-start | bytes 1572868
  66.4 42.7 %collective-permute-start.10 = (bf16[512,512]{1,0:T(8,128)(2,1)}, bf16[512,512]{1,0:T(8,128)(2,1)}, u32[]{:S(2)}, u32[]{:S(2)}) collective-permute-start(bf16[512,512]{1,0:T(8,128)(2,1)} %get-tuple-element.30), channel_id=1, source_target_pairs={{0,3},{1,0},{2,1},{3,2},{4,7},{5,4},{6,5},{7,6},{8,11},{9,8},{10,9... | collective-permute-start | bytes 1572872 | tf_op jit(solution)/shard_map/ppermute | solution.py:122
  68.5 40.6 %collective-permute-start.11 = (bf16[512,512]{1,0:T(8,128)(2,1)}, bf16[512,512]{1,0:T(8,128)(2,1)}, u32[]{:S(2)}, u32[]{:S(2)}) collective-permute-start(bf16[512,512]{1,0:T(8,128)(2,1)} %get-tuple-element.31), channel_id=1, source_target_pairs={{0,5},{1,6},{2,7},{3,4},{4,1},{5,2},{6,3},{7,0},{8,13},{9,14},{10,... | collective-permute-start | bytes 1572872 | tf_op jit(solution)/shard_map/ppermute | solution.py:122
  114.5 0.8 copy-start.3
  115.3 0.8 copy-start.4
  120.3 0.8 copy-start
